TPU v7x, 256 devices: a whole 4x4x8 slice. The times are simulated.
256 devices in a mesh: tm: 8 (over y, x_lo), rows: 32 (over x_hi, z, core).
Axes of the slice: x: 4 (x_hi: 2, x_lo: 2; x = x_hi * 2 + x_lo), y: 4, z: 8, core: 2. Of those that a mesh axis runs over, the one named last changes fastest.
Arguments:
- queries: bfloat16 [32, 256, 16, 1792], P('tm', 'rows'), may hold values from -60 to 60
- keys: bfloat16 [32, 256, 16, 1792], P('tm', 'rows'), may hold values from -6 to 6
- values: bfloat16 [32, 256, 16, 1792], P('tm', 'rows'), may hold values from -6 to 6
- out_grad: bfloat16 [32, 256, 16, 1792], P('tm', 'rows'), may hold values from -6 to 6
Outputs:
- query_grad: bfloat16 [32, 256, 16, 1792], P('tm', 'rows')
- key_grad: bfloat16 [32, 256, 16, 1792], P('tm', 'rows')
- value_grad: bfloat16 [32, 256, 16, 1792], P('tm', 'rows')
All inputs are finite; a program needn't handle non-finite values.
Results may differ from a plain program's by a relative error of at most 0.012.
Values may be sent and summed in bfloat16 or wider, within the bound.
A program may use at most 128 MiB of HBM per device.

v0:
```python
import math

import jax
import jax.numpy as jnp
from jax import lax
from jax.sharding import PartitionSpec as P

WW = 8
HEADS = 14
HEAD_DIM = 128


def passed_along(value, axis, by):
    size = lax.axis_size(axis)
    return lax.ppermute(value, axis, [(i, (i + by) % size) for i in range(size)])


def window_grads(query_w, key_w, value_w, grad_w):
    factor = 1.0 / math.sqrt(query_w.shape[-1])
    scores = (
        jnp.einsum("bhqd,bhkd->bhqk", query_w, key_w, preferred_element_type=jnp.float32) * factor
    )
    weights = jax.nn.softmax(scores, axis=-1)
    weights_b = weights.astype(jnp.bfloat16)
    attended = jnp.einsum("bhqk,bhkd->bhqd", weights_b, value_w, preferred_element_type=jnp.float32)
    row_dot = jnp.sum(grad_w.astype(jnp.float32) * attended, axis=-1, keepdims=True)
    weight_grad = jnp.einsum("bhqd,bhkd->bhqk", grad_w, value_w, preferred_element_type=jnp.float32)
    score_grad = (weights * (weight_grad - row_dot) * factor).astype(jnp.bfloat16)
    value_out = jnp.einsum(
        "bhqk,bhqd->bhkd", weights_b, grad_w, preferred_element_type=jnp.float32
    ).astype(jnp.bfloat16)
    query_out = jnp.einsum(
        "bhqk,bhkd->bhqd", score_grad, key_w, preferred_element_type=jnp.float32
    ).astype(jnp.bfloat16)
    key_out = jnp.einsum(
        "bhqk,bhqd->bhkd", score_grad, query_w, preferred_element_type=jnp.float32
    ).astype(jnp.bfloat16)
    return jnp.stack((query_out, key_out, value_out))


def forward_route(stacked):
    half_time = stacked.shape[1] // 2
    half_rows = stacked.shape[2] // 2
    row_slab = passed_along(stacked[:, :, :half_rows], "rows", -1)
    time_slab = passed_along(stacked[:, :half_time, half_rows:], "tm", -1)
    corner = passed_along(row_slab[:, :half_time], "tm", -1)
    top_half = jnp.concatenate(
        (stacked[:, half_time:, half_rows:], row_slab[:, half_time:]), axis=2
    )
    bottom_half = jnp.concatenate((time_slab, corner), axis=2)
    return jnp.concatenate((top_half, bottom_half), axis=1)


def backward_route(grads):
    half_time = grads.shape[1] // 2
    half_rows = grads.shape[2] // 2
    row_slab = passed_along(grads[:, :, half_rows:], "rows", 1)
    time_slab = passed_along(grads[:, half_time:, :half_rows], "tm", 1)
    corner = passed_along(row_slab[:, half_time:], "tm", 1)
    top_half = jnp.concatenate((corner, time_slab), axis=2)
    bottom_half = jnp.concatenate(
        (row_slab[:, :half_time], grads[:, :half_time, :half_rows]), axis=2
    )
    return jnp.concatenate((top_half, bottom_half), axis=1)


def shards(queries, keys, values, out_grad):
    stacked = jnp.stack((queries, keys, values, out_grad))
    shifted = forward_route(stacked)
    rolled = jnp.roll(shifted, -(WW // 2), axis=3)
    groups, frames, rows_here, columns, features = rolled.shape
    window_count = columns // WW
    length = frames * rows_here * WW
    windowed = rolled.reshape(groups, frames, rows_here, window_count, WW, HEADS, HEAD_DIM)
    windowed = windowed.transpose(0, 3, 5, 1, 2, 4, 6).reshape(
        groups, window_count, HEADS, length, HEAD_DIM
    )
    grads = window_grads(windowed[0], windowed[1], windowed[2], windowed[3])
    restored = grads.reshape(3, window_count, HEADS, frames, rows_here, WW, HEAD_DIM)
    restored = restored.transpose(0, 3, 4, 1, 5, 2, 6).reshape(
        3, frames, rows_here, columns, features
    )
    restored = jnp.roll(restored, WW // 2, axis=3)
    unshifted = backward_route(restored)
    return (unshifted[0], unshifted[1], unshifted[2])


def solution(mesh):
    return jax.shard_map(
        shards,
        mesh=mesh,
        in_specs=(
            P("tm", "rows", None, None),
            P("tm", "rows", None, None),
            P("tm", "rows", None, None),
            P("tm", "rows", None, None),
        ),
        out_specs=(
            P("tm", "rows", None, None),
            P("tm", "rows", None, None),
            P("tm", "rows", None, None),
        ),
        check_vma=False,
    )
```

profile of v0, /device:TPU:224, one launch (start us, length us, event | category | flops | bytes accessed | tf_op | source)
XLA Modules:
  0.0 246.7 jit_solution(18173439223349659303)
XLA Ops:
  0.6 4.0 %pad_maximum_fusion.8 = bf16[4,4,8,16,1792]{4,3,2,1,0:T(8,128)(2,1)S(1)} fusion(bf16[1,4,8,16,1792]{4,3,2,1,0:T(8,128)(2,1)} %bitcast.45, bf16[1,4,8,16,1792]{4,3,2,1,0:T(8,128)(2,1)} %bitcast.49, bf16[1,4,8,16,1792]{4,3,2,1,0:T(8,128)(2,1)} %bitcast.53, bf16[1,4,8,16,1792]{4,3,2,1,0:T(8,128)(2,1)} %bitcast.57), kind=kLoop, calls=%fused_computation.14 | loop fusion | flops 11010048 | bytes 14680064 | tf_op jit(solution)/shard_map/stack | solution.py:68
  5.1 0.5 collective-permute-start
  5.6 0.6 copy-done
  6.2 0.6 copy-done.1
  6.7 0.6 copy-done.2
  7.3 0.5 copy-done.3
  8.1 4.0 %collective-permute-start.1 = (bf16[4,2,4,16,1792]{4,3,2,1,0:T(8,128)(2,1)S(1)}, bf16[4,2,4,16,1792]{4,3,2,1,0:T(8,128)(2,1)S(1)}, u32[]{:S(2)}, u32[]{:S(2)}) collective-permute-start(bf16[4,2,4,16,1792]{4,3,2,1,0:T(8,128)(2,1)S(1)} %pad_maximum_fusion.10), channel_id=1, source_target_pairs={{0,224},{32,0},{64,32},{96,64},{128,96},{160,128},{192,160},{224,1... | collective-permute-start | bytes 5505032 | tf_op jit(solution)/shard_map/ppermute | solution.py:15
  12.1 33.9 %collective-permute-done = bf16[4,4,4,16,1792]{4,3,2,1,0:T(8,128)(2,1)S(1)} collective-permute-done((bf16[4,4,4,16,1792]{4,3,2,1,0:T(8,128)(2,1)S(1)}, bf16[4,4,4,16,1792]{4,3,2,1,0:T(8,128)(2,1)S(1)}, u32[]{:S(2)}, u32[]{:S(2)}) %collective-permute-start) | collective-permute-done | bytes 3670048 | tf_op jit(solution)/shard_map/ppermute | solution.py:15
  46.3 4.0 %collective-permute-start.2 = (bf16[4,2,4,16,1792]{4,3,2,1,0:T(8,128)(2,1)S(1)}, bf16[4,2,4,16,1792]{4,3,2,1,0:T(8,128)(2,1)S(1)}, u32[]{:S(2)}, u32[]{:S(2)}) collective-permute-start(bf16[4,2,4,16,1792]{4,3,2,1,0:T(8,128)(2,1)S(1)} %get-tuple-element.11), channel_id=1, source_target_pairs={{0,224},{32,0},{64,32},{96,64},{128,96},{160,128},{192,160},{224,1... | collective-permute-start | bytes 5505032 | tf_op jit(solution)/shard_map/ppermute | solution.py:15
  50.4 40.0 %collective-permute-done.1 = bf16[4,2,4,16,1792]{4,3,2,1,0:T(8,128)(2,1)S(1)} collective-permute-done((bf16[4,2,4,16,1792]{4,3,2,1,0:T(8,128)(2,1)S(1)}, bf16[4,2,4,16,1792]{4,3,2,1,0:T(8,128)(2,1)S(1)}, u32[]{:S(2)}, u32[]{:S(2)}) %collective-permute-start.1) | collective-permute-done | bytes 1835040 | tf_op jit(solution)/shard_map/ppermute | solution.py:15
  90.3 38.4 %collective-permute-done.2 = bf16[4,2,4,16,1792]{4,3,2,1,0:T(8,128)(2,1)S(1)} collective-permute-done((bf16[4,2,4,16,1792]{4,3,2,1,0:T(8,128)(2,1)S(1)}, bf16[4,2,4,16,1792]{4,3,2,1,0:T(8,128)(2,1)S(1)}, u32[]{:S(2)}, u32[]{:S(2)}) %collective-permute-start.2) | collective-permute-done | bytes 1835040 | tf_op jit(solution)/shard_map/ppermute | solution.py:15
  128.8 3.7 %fusion.5 = bf16[4,4,8,16,1792]{4,3,2,1,0:T(8,128)(2,1)} fusion(bf16[1,4,8,16,1792]{4,3,2,1,0:T(8,128)(2,1)S(1)} %bitcast.47, bf16[1,4,8,16,1792]{4,3,2,1,0:T(8,128)(2,1)S(1)} %bitcast.51, bf16[1,4,8,16,1792]{4,3,2,1,0:T(8,128)(2,1)S(1)} %bitcast.55, bf16[1,4,8,16,1792]{4,3,2,1,0:T(8,128)(2,1)S(1)} %bitcast.59, ...), kind=kLoop, calls=%fused_computation.11 | loop fusion | flops 22020096 | bytes 20185088 | tf_op jit(solution)/shard_map/concatenate | solution.py:51
  132.5 9.8 %slice.95 = bf16[4,4,8,12,1792]{4,3,2,1,0:T(8,128)(2,1)} slice(bf16[4,4,8,16,1792]{4,3,2,1,0:T(8,128)(2,1)} %fusion.5), slice={[0:4], [0:4], [0:8], [4:16], [0:1792]} | slice | bytes 11010048 | tf_op jit(solution)/shard_map/jit(_roll_static)/slice | solution.py:70
  142.3 7.0 %copy_bitcast_fusion = bf16[4,2,14,4,8,8,128]{6,5,4,3,2,1,0:T(8,128)(2,1)S(1)} fusion(bf16[4,2,4,16,1792]{4,3,2,1,0:T(8,128)(2,1)S(1)} %collective-permute-done.2, bf16[4,2,4,16,1792]{4,3,2,1,0:T(8,128)(2,1)S(1)} %collective-permute-done.1, bf16[4,2,4,16,1792]{4,3,2,1,0:T(8,128)(2,1)S(1)} %get-tuple-element.10, bf16[1,4,8,16,1792]{4,3,2,1,0:T(8,128)(2,1)S(1)} %bitcast.48, ...), kind=kLoop, calls=%fused_computation.15 | loop fusion | flops 58720256 | bytes 25690112 | tf_op jit(solution)/shard_map/transpose | solution.py:75
  149.3 3.4 %fusion.18 = (bf16[1,2,14,4,8,8,128]{6,5,4,3,2,1,0:T(8,128)(2,1)}, bf16[1,2,14,4,8,8,128]{6,5,4,3,2,1,0:T(8,128)(2,1)}, bf16[1,2,14,4,8,8,128]{6,5,4,3,2,1,0:T(8,128)(2,1)S(1)}, bf16[1,2,14,4,8,8,128]{6,5,4,3,2,1,0:T(8,128)(2,1)}) fusion(bf16[4,2,14,4,8,8,128]{6,5,4,3,2,1,0:T(8,128)(2,1)S(1)} %copy_bitcast_fusion), kind=kLoop, calls=%fused_computation.44 | loop fusion | bytes 14680064 | tf_op jit(solution)/shard_map/slice | solution.py:78
  152.7 6.8 %fusion.21 = (f32[2,14,256]{2,1,0:T(8,128)S(1)}, f32[2,14,256,256]{2,3,1,0:T(8,128)}) fusion(bf16[2,14,256,128]{3,2,1,0:T(8,128)(2,1)} %bitcast.63, bf16[2,14,256,128]{3,2,1,0:T(8,128)(2,1)S(1)} %bitcast.61), kind=kOutput, calls=%fused_computation.47 | convolution fusion | flops 475267328 | bytes 11038720 | tf_op jit(solution)/shard_map/sub | solution.py:23
  159.5 4.1 %fusion.12 = bf16[2,14,256,256]{2,3,1,0:T(8,128)(2,1)S(1)} fusion(f32[2,14,256,256]{2,3,1,0:T(8,128)} %get-tuple-element.15, f32[2,14,256]{2,1,0:T(8,128)S(1)} %get-tuple-element.14), kind=kLoop, calls=%fused_computation.32 | loop fusion | flops 3670016 | bytes 11038720 | tf_op jit(solution)/shard_map/convert_element_type | solution.py:24
  163.6 1.1 convolution_convert_fusion
  165.1 2.0 multiply_reduce_fusion.1
  167.5 1.4 multiply_convert_fusion
  169.0 1.1 convolution_convert_fusion.1
  170.1 1.2 convolution_convert_fusion.2
  171.3 4.1 %copy_bitcast_fusion.1 = bf16[3,4,8,16,1792]{4,3,2,1,0:T(8,128)(2,1)S(1)} fusion(bf16[1,2,14,4,8,8,128]{6,5,4,3,2,1,0:T(8,128)(2,1)S(1)} %bitcast.70, bf16[1,2,14,4,8,8,128]{6,5,4,3,2,1,0:T(8,128)(2,1)S(1)} %bitcast.71, bf16[1,2,14,4,8,8,128]{6,5,4,3,2,1,0:T(8,128)(2,1)S(1)} %bitcast.72), kind=kLoop, calls=%fused_computation.26 | loop fusion | flops 5505024 | bytes 11010048 | tf_op jit(solution)/shard_map/reshape | solution.py:80
  175.4 0.8 slice.100
  176.2 1.2 fusion.13
  178.1 2.2 collective-permute-start.5
  180.3 29.7 %collective-permute-done.3 = bf16[3,4,4,16,1792]{4,3,2,1,0:T(8,128)(2,1)S(1)} collective-permute-done((bf16[3,4,4,16,1792]{4,3,2,1,0:T(8,128)(2,1)S(1)}, bf16[3,4,4,16,1792]{4,3,2,1,0:T(8,128)(2,1)S(1)}, u32[]{:S(2)}, u32[]{:S(2)}) %collective-permute-start.3) | collective-permute-done | bytes 2752544 | tf_op jit(solution)/shard_map/ppermute | solution.py:15
  210.2 2.2 collective-permute-start.4
  212.4 0.7 collective-permute-done.5
  213.1 29.7 %collective-permute-done.4 = bf16[3,2,4,16,1792]{4,3,2,1,0:T(8,128)(2,1)S(1)} collective-permute-done((bf16[3,2,4,16,1792]{4,3,2,1,0:T(8,128)(2,1)S(1)}, bf16[3,2,4,16,1792]{4,3,2,1,0:T(8,128)(2,1)S(1)}, u32[]{:S(2)}, u32[]{:S(2)}) %collective-permute-start.4) | collective-permute-done | bytes 1376288 | tf_op jit(solution)/shard_map/ppermute | solution.py:15
  242.8 1.3 fusion.8
  244.1 2.6 %slice_bitcast_fusion = (bf16[4,8,16,1792]{3,2,1,0:T(8,128)(2,1)}, bf16[4,8,16,1792]{3,2,1,0:T(8,128)(2,1)}, bf16[4,8,16,1792]{3,2,1,0:T(8,128)(2,1)}) fusion(bf16[3,4,8,16,1792]{4,3,2,1,0:T(8,128)(2,1)S(1)} %fusion.8), kind=kLoop, calls=%fused_computation.34 | loop fusion | bytes 11010048 | tf_op jit(solution)/shard_map/squeeze | solution.py:85
  (21 shorter events, 2.6 us)
Async XLA Ops:
  4.7 1.5 copy-start
  4.7 2.0 copy-start.1
  4.7 2.6 %copy-start.2 = (bf16[4,8,16,1792]{3,2,1,0:T(8,128)(2,1)S(1)}, bf16[4,8,16,1792]{3,2,1,0:T(8,128)(2,1)}, u32[]{:S(2)}) copy-start(bf16[4,8,16,1792]{3,2,1,0:T(8,128)(2,1)} %param.5) | copy-start | bytes 5505028
  4.7 3.1 %copy-start.3 = (bf16[4,8,16,1792]{3,2,1,0:T(8,128)(2,1)S(1)}, bf16[4,8,16,1792]{3,2,1,0:T(8,128)(2,1)}, u32[]{:S(2)}) copy-start(bf16[4,8,16,1792]{3,2,1,0:T(8,128)(2,1)} %param.4) | copy-start | bytes 5505028
  5.1 40.9 %collective-permute-start = (bf16[4,4,4,16,1792]{4,3,2,1,0:T(8,128)(2,1)S(1)}, bf16[4,4,4,16,1792]{4,3,2,1,0:T(8,128)(2,1)S(1)}, u32[]{:S(2)}, u32[]{:S(2)}) collective-permute-start(bf16[4,4,4,16,1792]{4,3,2,1,0:T(8,128)(2,1)S(1)} %slice.92), channel_id=1, source_target_pairs={{0,31},{1,0},{2,1},{3,2},{4,3},{5,4},{6,5},{7,6},{8,7},{9,8},{10,9... | collective-permute-start | bytes 11010056 | tf_op jit(solution)/shard_map/ppermute | solution.py:15
  8.1 82.3 %collective-permute-start.1 = (bf16[4,2,4,16,1792]{4,3,2,1,0:T(8,128)(2,1)S(1)}, bf16[4,2,4,16,1792]{4,3,2,1,0:T(8,128)(2,1)S(1)}, u32[]{:S(2)}, u32[]{:S(2)}) collective-permute-start(bf16[4,2,4,16,1792]{4,3,2,1,0:T(8,128)(2,1)S(1)} %pad_maximum_fusion.10), channel_id=1, source_target_pairs={{0,224},{32,0},{64,32},{96,64},{128,96},{160,128},{192,160},{224,1... | collective-permute-start | bytes 5505032 | tf_op jit(solution)/shard_map/ppermute | solution.py:15
  46.3 82.4 %collective-permute-start.2 = (bf16[4,2,4,16,1792]{4,3,2,1,0:T(8,128)(2,1)S(1)}, bf16[4,2,4,16,1792]{4,3,2,1,0:T(8,128)(2,1)S(1)}, u32[]{:S(2)}, u32[]{:S(2)}) collective-permute-start(bf16[4,2,4,16,1792]{4,3,2,1,0:T(8,128)(2,1)S(1)} %get-tuple-element.11), channel_id=1, source_target_pairs={{0,224},{32,0},{64,32},{96,64},{128,96},{160,128},{192,160},{224,1... | collective-permute-start | bytes 5505032 | tf_op jit(solution)/shard_map/ppermute | solution.py:15
  159.5 4.1 %copy-start.5 = (bf16[1,2,14,4,8,8,128]{6,5,4,3,2,1,0:T(8,128)(2,1)S(1)}, bf16[1,2,14,4,8,8,128]{6,5,4,3,2,1,0:T(8,128)(2,1)}, u32[]{:S(2)}) copy-start(bf16[1,2,14,4,8,8,128]{6,5,4,3,2,1,0:T(8,128)(2,1)} %get-tuple-element.4) | copy-start | bytes 5505028
  163.6 1.5 copy-start.6
  163.6 3.5 %slice-start = ((s8[7340032]{0:T(1024)(128)(4,1)}), s8[4194304]{0:T(1024)(128)(4,1)S(1)}, s32[]{:S(2)}) async-start(s8[7340032]{0:T(1024)(128)(4,1)} %bitcast.68), calls=%async_computation | async-start | bytes 8388608
  165.1 2.4 slice-start.1
  167.5 1.5 copy-start.4
  177.4 32.6 %collective-permute-start.3 = (bf16[3,4,4,16,1792]{4,3,2,1,0:T(8,128)(2,1)S(1)}, bf16[3,4,4,16,1792]{4,3,2,1,0:T(8,128)(2,1)S(1)}, u32[]{:S(2)}, u32[]{:S(2)}) collective-permute-start(bf16[3,4,4,16,1792]{4,3,2,1,0:T(8,128)(2,1)S(1)} %fusion.13), channel_id=1, source_target_pairs={{0,1},{1,2},{2,3},{3,4},{4,5},{5,6},{6,7},{7,8},{8,9},{9,10},{10,1... | collective-permute-start | bytes 8257544 | tf_op jit(solution)/shard_map/ppermute | solution.py:15
  178.1 35.0 %collective-permute-start.5 = (bf16[3,2,4,16,1792]{4,3,2,1,0:T(8,128)(2,1)S(1)}, bf16[3,2,4,16,1792]{4,3,2,1,0:T(8,128)(2,1)S(1)}, u32[]{:S(2)}, u32[]{:S(2)}) collective-permute-start(bf16[3,2,4,16,1792]{4,3,2,1,0:T(8,128)(2,1)S(1)} %fusion.14), channel_id=1, source_target_pairs={{0,32},{32,64},{64,96},{96,128},{128,160},{160,192},{192,224},{224... | collective-permute-start | bytes 4128776 | tf_op jit(solution)/shard_map/ppermute | solution.py:15
  210.2 32.6 %collective-permute-start.4 = (bf16[3,2,4,16,1792]{4,3,2,1,0:T(8,128)(2,1)S(1)}, bf16[3,2,4,16,1792]{4,3,2,1,0:T(8,128)(2,1)S(1)}, u32[]{:S(2)}, u32[]{:S(2)}) collective-permute-start(bf16[3,2,4,16,1792]{4,3,2,1,0:T(8,128)(2,1)S(1)} %get-tuple-element.12), channel_id=1, source_target_pairs={{0,32},{32,64},{64,96},{96,128},{128,160},{160,192},{192,224},{224... | collective-permute-start | bytes 4128776 | tf_op jit(solution)/shard_map/ppermute | solution.py:15
where the time goes:
time: 247 us
  waiting for transfers between devices  172 us (70%)
  other arithmetic  26.3 us (11%)
  local copies, waits for them, and re-layouts  20.5 us (8%)
  matrix products  13.6 us (6%)
  starting transfers between devices  13.1 us (5%)
    ppermute x6, waiting for transfers between devices, passed_along(): lax.ppermute(value, axis, [(i, (i + by) % size) for i in range(size)])  172 us
    ppermute x6, starting transfers between devices, passed_along(): lax.ppermute(value, axis, [(i, (i + by) % size) for i in range(size)])  13.1 us
    slice x1, local copies, waits for them, and re-layouts, shards(): rolled = jnp.roll(shifted, -(WW // 2), axis=3)  9.81 us
    transpose x1, other arithmetic, shards(): windowed.transpose(0, 3, 5, 1, 2, 4, 6)  6.99 us
    sub x1, matrix products, window_grads(): weights = jax.nn.softmax(scores, axis=-1)  6.83 us
  transfers between devices with their start and end apart: 6, of which 6 were waited for; matrix products, arithmetic and copies ran while one was open for 1% of the time, Pallas kernels for 0%

commit v1 on v0

v1 whole, which is shorter than its diff:
```python
import functools
import math

import jax
import jax.numpy as jnp
from jax import lax
from jax.experimental import pallas as pl
from jax.experimental.pallas import tpu as pltpu
from jax.sharding import PartitionSpec as P

MESH = pl.DeviceIdType.MESH
HEAD_DIM = 128
WW = 8
AHEAD = 3
LAG = 3

PER_HALF = 12
OWN_ROLE = (2, 0)


def kernel(tm, rows, q_ref, k_ref, v_ref, g_ref, dq_ref, dk_ref, dv_ref, blocks, stat_out, stat_in, dq_part, dkv,
           dq_in, dq_sum, sems):
    t, r = lax.axis_index("tm"), lax.axis_index("rows")
    frames, rows_here, cols, features = q_ref.shape
    heads = features // HEAD_DIM
    fh, rh = frames // 2, rows_here // 2
    factor = 1.0 / math.sqrt(HEAD_DIM)
    side = rows // 2
    seam_before = 1 - (r % side + side - 1) // side
    seam_after = 1 - ((r + 1) % side + side - 1) // side
    tp, tn = (t + 1) % tm, (t + tm - 1) % tm
    rp, rn = (r + 1) % rows, (r + rows - 1) % rows

    (fwd_send, fwd_recv, load_sem, stat_send, stat_recv, out_send, dq_recv, dkv_recv, dkv_store, dq_store) = (
        sems.at[i] for i in range(10)
    )

    def quad(ref, late_frames, late_rows, h):
        return ref.at[
            pl.ds(late_frames * fh, fh),
            pl.ds(late_rows * rh, rh),
            :,
            pl.ds(pl.multiple_of(h * HEAD_DIM, HEAD_DIM), HEAD_DIM),
        ]

    def send(src, dst, send_sem, recv_sem, device):
        pltpu.make_async_remote_copy(
            src_ref=src, dst_ref=dst, send_sem=send_sem, recv_sem=recv_sem, device_id=device, device_id_type=MESH
        ).start()

    def wait_bytes(ref, sem):
        pltpu.make_async_copy(ref, ref, sem).wait()

    barrier = pltpu.get_barrier_semaphore()
    around = [(tp, r), (tn, r), (t, rp), (t, rn), (tp, rp), (tp, rn), (tn, rp), (tn, rn)]
    for device in around:
        pl.semaphore_signal(barrier, inc=1, device_id=device, device_id_type=MESH)

    def load_own(h, carry):
        for half in range(2):
            base = half * PER_HALF
            role = OWN_ROLE[half]
            for ref, slot in ((q_ref, role), (g_ref, 4 + role), (k_ref, 8), (v_ref, 10)):
                pltpu.make_async_copy(quad(ref, half, 1, h), blocks.at[h, base + slot], load_sem.at[h]).start()
        return carry

    lax.fori_loop(0, heads, load_own, 0)
    pl.semaphore_wait(barrier, len(around))

    def send_inputs(h):
        sem = (fwd_send.at[h], fwd_recv.at[h])
        for ref, off in ((q_ref, 0), (g_ref, 4)):
            send(quad(ref, 1, 1, h), blocks.at[h, off + 0], *sem, (tp, r))
            send(quad(ref, 0, 1, h), blocks.at[h, PER_HALF + off + 2], *sem, (tn, r))
            send(quad(ref, 1, 0, h), blocks.at[h, off + 1], *sem, (tp, rn))
            send(quad(ref, 0, 0, h), blocks.at[h, PER_HALF + off + 3], *sem, (tn, rn))
            send(quad(ref, 1, 0, h), blocks.at[h, PER_HALF + off + 1], *sem, (t, rn))
            send(quad(ref, 0, 0, h), blocks.at[h, off + 3], *sem, (t, rn))
        for ref, off in ((k_ref, 9), (v_ref, 11)):
            send(
                quad(ref, 1, 0, h),
                blocks.at[h, (1 - seam_before) * PER_HALF + off],
                *sem,
                ((t + seam_before) % tm, rn),
            )
            send(
                quad(ref, 0, 0, h),
                blocks.at[h, seam_before * PER_HALF + off],
                *sem,
                ((t + tm - seam_before) % tm, rn),
            )

    def send_stats(h):
        sem = (stat_send.at[h], stat_recv.at[h])
        send(stat_out.at[h, 1], stat_in.at[h, 0], *sem, (tp, r))
        send(stat_out.at[h, 0], stat_in.at[h, 1], *sem, (tn, r))

    def send_outputs(h):
        sem = (out_send.at[h], dq_recv.at[h])
        send(dq_part.at[h, 1, 2], dq_in.at[h, 5], *sem, (tp, r))
        send(dq_part.at[h, 0, 0], dq_in.at[h, 4], *sem, (tn, r))
        send(dq_part.at[h, 1, 3], dq_in.at[h, 2], *sem, (tp, rp))
        send(dq_part.at[h, 0, 1], dq_in.at[h, 1], *sem, (tn, rp))
        send(dq_part.at[h, 1, 1], dq_in.at[h, 0], *sem, (t, rp))
        send(dq_part.at[h, 0, 3], dq_in.at[h, 3], *sem, (t, rp))
        sem = (out_send.at[h], dkv_recv.at[h])
        for kind, ref in enumerate((dk_ref, dv_ref)):
            send(
                dkv.at[h, kind, 1, 1], quad(ref, 1 - seam_after, 0, h), *sem, ((t + seam_after) % tm, rp)
            )
            send(
                dkv.at[h, kind, 0, 1], quad(ref, seam_after, 0, h), *sem, ((t + tm - seam_after) % tm, rp)
            )
            for half in range(2):
                pltpu.make_async_copy(dkv.at[h, kind, half, 0], quad(ref, half, 1, h), dkv_store.at[h]).start()

    key_col = lax.broadcasted_iota(jnp.int32, (cols, HEAD_DIM), 0)
    query_col = lax.broadcasted_iota(jnp.int32, (cols, HEAD_DIM), 1)
    shifted = cols - WW // 2
    apart = ((key_col + shifted) ^ (query_col + shifted)) & WW
    bias = jnp.where(apart == 0, 0.0, -1e30).astype(jnp.float32)

    tokens = fh * rh * cols

    def block(h, index, count=1):
        return blocks[h, pl.ds(index, count)].reshape(count * tokens, HEAD_DIM)

    def scores_of(keys, queries):
        scores = lax.dot_general(keys, queries, (((1,), (1,)), ((), ())), preferred_element_type=jnp.float32)
        scores = (scores * factor).reshape(2 * tokens // cols, cols, tokens) + bias[None]
        return scores.reshape(2 * tokens, tokens)

    def first_stage(h):
        for half in range(2):
            base = half * PER_HALF
            keys, values = block(h, base + 8, 2), block(h, base + 10, 2)
            for role in range(4):
                scores = scores_of(keys, block(h, base + role))
                dprobs = lax.dot_general(
                    values, block(h, base + 4 + role), (((1,), (1,)), ((), ())), preferred_element_type=jnp.float32
                )
                top = jnp.max(scores, axis=0, keepdims=True)
                weights = jnp.exp(scores - top)
                total = jnp.sum(weights, axis=0, keepdims=True)
                dots = jnp.sum(weights * dprobs, axis=0, keepdims=True)
                lanes = pl.ds(role * tokens, tokens)
                stat_out[h, half, 0:1, lanes] = top + jnp.log(total)
                stat_out[h, half, 1:2, lanes] = dots / total

    def second_stage(h):
        for half in range(2):
            base = half * PER_HALF
            keys, values = block(h, base + 8, 2), block(h, base + 10, 2)
            dk = jnp.zeros((2 * tokens, HEAD_DIM), jnp.float32)
            dv = jnp.zeros((2 * tokens, HEAD_DIM), jnp.float32)
            for role in range(4):
                lanes = pl.ds(role * tokens, tokens)
                mine, other = stat_out[h, half, 0:1, lanes], stat_in[h, half, 0:1, lanes]
                norm = jnp.maximum(mine, other) + jnp.log(1.0 + jnp.exp(-jnp.abs(mine - other)))
                row_dot = stat_out[h, half, 1:2, lanes] * jnp.exp(mine - norm)
                row_dot += stat_in[h, half, 1:2, lanes] * jnp.exp(other - norm)
                queries, grads = block(h, base + role), block(h, base + 4 + role)
                probs = jnp.exp(scores_of(keys, queries) - norm)
                dprobs = lax.dot_general(
                    values, grads, (((1,), (1,)), ((), ())), preferred_element_type=jnp.float32
                )
                dscores = (probs * (dprobs - row_dot) * factor).astype(jnp.bfloat16)
                dv += jnp.dot(probs.astype(jnp.bfloat16), grads, preferred_element_type=jnp.float32)
                dk += jnp.dot(dscores, queries, preferred_element_type=jnp.float32)
                dq = lax.dot_general(dscores, keys, (((0,), (0,)), ((), ())), preferred_element_type=jnp.float32)
                dq_part[h, half, role] = dq.astype(jnp.bfloat16).reshape(fh, rh, cols, HEAD_DIM)
            dkv[h, 0, half] = dk.astype(jnp.bfloat16).reshape(2, fh, rh, cols, HEAD_DIM)
            dkv[h, 1, half] = dv.astype(jnp.bfloat16).reshape(2, fh, rh, cols, HEAD_DIM)

    for h in range(min(AHEAD, heads)):
        send_inputs(h)

    def step(i, carry):
        @pl.when(i < heads)
        def _():
            wait_bytes(blocks.at[i, pl.ds(0, 8)], load_sem.at[i])
            wait_bytes(blocks.at[i, pl.ds(0, 16)], fwd_recv.at[i])

        @pl.when(i + AHEAD < heads)
        def _():
            send_inputs(i + AHEAD)

        @pl.when(i > LAG)
        def _():
            send_outputs(i - LAG - 1)

        @pl.when(i < heads)
        def _():
            first_stage(i)

        @pl.when((i >= LAG) & (i < heads + LAG))
        def _():
            wait_bytes(stat_in.at[i - LAG], stat_recv.at[i - LAG])
            second_stage(i - LAG)

        @pl.when(i < heads)
        def _():
            send_stats(i)

        return carry

    lax.fori_loop(0, heads + LAG + 1, step, 0)

    def finish(h, carry):
        wait_bytes(dq_in.at[h], dq_recv.at[h])
        f32 = jnp.float32
        dq_sum[h, 1, 0] = (dq_in[h, 0].astype(f32) + dq_in[h, 1].astype(f32)).astype(jnp.bfloat16)
        dq_sum[h, 0, 0] = (dq_in[h, 2].astype(f32) + dq_in[h, 3].astype(f32)).astype(jnp.bfloat16)
        dq_sum[h, 1, 1] = (dq_in[h, 4].astype(f32) + dq_part[h, 1, 0].astype(f32)).astype(jnp.bfloat16)
        dq_sum[h, 0, 1] = (dq_in[h, 5].astype(f32) + dq_part[h, 0, 2].astype(f32)).astype(jnp.bfloat16)
        for half in range(2):
            for late_rows in range(2):
                pltpu.make_async_copy(
                    dq_sum.at[h, half, late_rows], quad(dq_ref, half, late_rows, h), dq_store.at[h]
                ).start()
        return carry

    lax.fori_loop(0, heads, finish, 0)

    def drain(h, carry):
        wait_bytes(blocks.at[h, pl.ds(0, 16)], fwd_send.at[h])
        wait_bytes(stat_out.at[h], stat_send.at[h])
        wait_bytes(blocks.at[h, pl.ds(0, 10)], out_send.at[h])
        wait_bytes(blocks.at[h, pl.ds(0, 4)], dkv_recv.at[h])
        wait_bytes(blocks.at[h, pl.ds(0, 4)], dkv_store.at[h])
        wait_bytes(blocks.at[h, pl.ds(0, 4)], dq_store.at[h])
        return carry

    lax.fori_loop(0, heads, drain, 0)


def solution(mesh):
    tm, rows = mesh.shape["tm"], mesh.shape["rows"]

    def shards(queries, keys, values, out_grad):
        frames, rows_here, cols, features = queries.shape
        heads = features // HEAD_DIM
        fh, rh = frames // 2, rows_here // 2
        tokens = fh * rh * cols
        quadrant = (fh, rh, cols, HEAD_DIM)
        bf16 = jnp.bfloat16
        hbm = pl.BlockSpec(memory_space=pl.ANY)
        out = jax.ShapeDtypeStruct(queries.shape, bf16)
        return pl.pallas_call(
            functools.partial(kernel, tm, rows),
            out_shape=(out, out, out),
            in_specs=[hbm] * 4,
            out_specs=(hbm, hbm, hbm),
            scratch_shapes=[
                pltpu.VMEM((heads, 2 * PER_HALF, *quadrant), bf16),
                pltpu.VMEM((heads, 2, 2, 4 * tokens), jnp.float32),
                pltpu.VMEM((heads, 2, 2, 4 * tokens), jnp.float32),
                pltpu.VMEM((heads, 2, 4, *quadrant), bf16),
                pltpu.VMEM((heads, 2, 2, 2, *quadrant), bf16),
                pltpu.VMEM((heads, 6, *quadrant), bf16),
                pltpu.VMEM((heads, 2, 2, *quadrant), bf16),
                pltpu.SemaphoreType.DMA((10, heads)),
            ],
            compiler_params=pltpu.CompilerParams(
                collective_id=0, has_side_effects=True, vmem_limit_bytes=60 * 1024 * 1024
            ),
        )(queries, keys, values, out_grad)

    spec = P("tm", "rows", None, None)
    return jax.shard_map(
        shards, mesh=mesh, in_specs=(spec,) * 4, out_specs=(spec,) * 3, check_vma=False
    )
```

time: 247 us -> 142 us (0.57)
  the two profiles are of different devices: /device:TPU:224 before, /device:TPU:4 now
where the time goes in v1:
time: 142 us
  Pallas kernels  135 us (95%)
  local copies, waits for them, and re-layouts  6.4 us (5%)
    pallas_call x1, Pallas kernels, shards(): pl.pallas_call(functools.partial(kernel, tm, rows), out_shape=(out, out,...  135 us
    unnamed x7, local copies, waits for them, and re-layouts  6.4 us

profile of v1, /device:TPU:4, one launch (start us, length us, event | category | flops | bytes accessed | tf_op | source)
XLA Modules:
  0.0 142.2 jit_solution(18155172295978959153)
XLA Ops:
  0.6 135.1 %shard_map.67 = (bf16[4,8,16,1792]{3,2,1,0:T(8,128)(2,1)}, bf16[4,8,16,1792]{3,2,1,0:T(8,128)(2,1)}, bf16[4,8,16,1792]{3,2,1,0:T(8,128)(2,1)}) custom-call(bf16[4,8,16,1792]{3,2,1,0:T(8,128)(2,1)} %q_ref.1, bf16[4,8,16,1792]{3,2,1,0:T(8,128)(2,1)} %k_ref.1, bf16[4,8,16,1792]{3,2,1,0:T(8,128)(2,1)} %v_ref.1, bf16[4,8,16,1792]{3,2,1,0:T(8,128)(2,1)} %g_ref.1), custom_call_target="tpu_custom_call" | custom-call | tf_op jit(solution)/shard_map/pallas_call | solution.py:249
  135.8 0.0 copy-start.1
  135.8 3.0 %copy.10 = bf16[4,8,16,1792]{3,2,1,0:T(8,128)(2,1)} copy(bf16[4,8,16,1792]{3,2,1,0:T(8,128)(2,1)} %get-tuple-element.6) | data formatting | bytes 3670016
  138.8 0.0 copy-done.1
  138.8 0.0 copy-start
  138.8 1.2 copy.11
  140.0 0.9 copy-done
  140.9 1.2 copy.12
Async XLA Ops:
  135.8 3.0 %copy-start.1 = (bf16[4,8,16,1792]{3,2,1,0:T(8,128)(2,1)S(1)}, bf16[4,8,16,1792]{3,2,1,0:T(8,128)(2,1)}, u32[]{:S(2)}) copy-start(bf16[4,8,16,1792]{3,2,1,0:T(8,128)(2,1)} %get-tuple-element.7) | copy-start | bytes 5505028
  138.8 2.2 %copy-start = (bf16[4,8,16,1792]{3,2,1,0:T(8,128)(2,1)S(1)}, bf16[4,8,16,1792]{3,2,1,0:T(8,128)(2,1)}, u32[]{:S(2)}) copy-start(bf16[4,8,16,1792]{3,2,1,0:T(8,128)(2,1)} %get-tuple-element.8) | copy-start | bytes 5505028

commit v2 on v1

--- a/solution.py
+++ b/solution.py
@@ -19,7 +19,7 @@
 
 
 def kernel(tm, rows, q_ref, k_ref, v_ref, g_ref, dq_ref, dk_ref, dv_ref, blocks, stat_out, stat_in, dq_part, dkv,
-           dq_in, dq_sum, sems):
+           dq_in, sems):
     t, r = lax.axis_index("tm"), lax.axis_index("rows")
     frames, rows_here, cols, features = q_ref.shape
     heads = features // HEAD_DIM
@@ -31,8 +31,8 @@
     tp, tn = (t + 1) % tm, (t + tm - 1) % tm
     rp, rn = (r + 1) % rows, (r + rows - 1) % rows
 
-    (fwd_send, fwd_recv, load_sem, stat_send, stat_recv, out_send, dq_recv, dkv_recv, dkv_store, dq_store) = (
-        sems.at[i] for i in range(10)
+    (fwd_send, fwd_recv, load_sem, stat_send, stat_recv, out_send, dq_recv, dkv_recv) = (
+        sems.at[i] for i in range(8)
     )
 
     def quad(ref, late_frames, late_rows, h):
@@ -42,6 +42,10 @@
             :,
             pl.ds(pl.multiple_of(h * HEAD_DIM, HEAD_DIM), HEAD_DIM),
         ]
+
+    def put(ref, late_frames, late_rows, h, value):
+        lanes = pl.ds(pl.multiple_of(h * HEAD_DIM, HEAD_DIM), HEAD_DIM)
+        ref[pl.ds(late_frames * fh, fh), pl.ds(late_rows * rh, rh), :, lanes] = value
 
     def send(src, dst, send_sem, recv_sem, device):
         pltpu.make_async_remote_copy(
@@ -105,14 +109,8 @@
         send(dq_part.at[h, 0, 3], dq_in.at[h, 3], *sem, (t, rp))
         sem = (out_send.at[h], dkv_recv.at[h])
         for kind, ref in enumerate((dk_ref, dv_ref)):
-            send(
-                dkv.at[h, kind, 1, 1], quad(ref, 1 - seam_after, 0, h), *sem, ((t + seam_after) % tm, rp)
-            )
-            send(
-                dkv.at[h, kind, 0, 1], quad(ref, seam_after, 0, h), *sem, ((t + tm - seam_after) % tm, rp)
-            )
-            for half in range(2):
-                pltpu.make_async_copy(dkv.at[h, kind, half, 0], quad(ref, half, 1, h), dkv_store.at[h]).start()
+            send(dkv.at[h, kind, 1], quad(ref, 1 - seam_after, 0, h), *sem, ((t + seam_after) % tm, rp))
+            send(dkv.at[h, kind, 0], quad(ref, seam_after, 0, h), *sem, ((t + tm - seam_after) % tm, rp))
 
     key_col = lax.broadcasted_iota(jnp.int32, (cols, HEAD_DIM), 0)
     query_col = lax.broadcasted_iota(jnp.int32, (cols, HEAD_DIM), 1)
@@ -169,8 +167,10 @@
                 dk += jnp.dot(dscores, queries, preferred_element_type=jnp.float32)
                 dq = lax.dot_general(dscores, keys, (((0,), (0,)), ((), ())), preferred_element_type=jnp.float32)
                 dq_part[h, half, role] = dq.astype(jnp.bfloat16).reshape(fh, rh, cols, HEAD_DIM)
-            dkv[h, 0, half] = dk.astype(jnp.bfloat16).reshape(2, fh, rh, cols, HEAD_DIM)
-            dkv[h, 1, half] = dv.astype(jnp.bfloat16).reshape(2, fh, rh, cols, HEAD_DIM)
+            for kind, (ref, total) in enumerate(((dk_ref, dk), (dv_ref, dv))):
+                total = total.astype(jnp.bfloat16).reshape(2, fh, rh, cols, HEAD_DIM)
+                put(ref, half, 1, h, total[0])
+                dkv[h, kind, half] = total[1]
 
     for h in range(min(AHEAD, heads)):
         send_inputs(h)
@@ -208,16 +208,15 @@
 
     def finish(h, carry):
         wait_bytes(dq_in.at[h], dq_recv.at[h])
-        f32 = jnp.float32
-        dq_sum[h, 1, 0] = (dq_in[h, 0].astype(f32) + dq_in[h, 1].astype(f32)).astype(jnp.bfloat16)
-        dq_sum[h, 0, 0] = (dq_in[h, 2].astype(f32) + dq_in[h, 3].astype(f32)).astype(jnp.bfloat16)
-        dq_sum[h, 1, 1] = (dq_in[h, 4].astype(f32) + dq_part[h, 1, 0].astype(f32)).astype(jnp.bfloat16)
-        dq_sum[h, 0, 1] = (dq_in[h, 5].astype(f32) + dq_part[h, 0, 2].astype(f32)).astype(jnp.bfloat16)
-        for half in range(2):
-            for late_rows in range(2):
-                pltpu.make_async_copy(
-                    dq_sum.at[h, half, late_rows], quad(dq_ref, half, late_rows, h), dq_store.at[h]
-                ).start()
+        own = dq_part.at[h]
+        for half, late_rows, first, second in (
+            (1, 0, dq_in.at[h, 0], dq_in.at[h, 1]),
+            (0, 0, dq_in.at[h, 2], dq_in.at[h, 3]),
+            (1, 1, dq_in.at[h, 4], own.at[1, 0]),
+            (0, 1, dq_in.at[h, 5], own.at[0, 2]),
+        ):
+            total = first[...].astype(jnp.float32) + second[...].astype(jnp.float32)
+            put(dq_ref, half, late_rows, h, total.astype(jnp.bfloat16))
         return carry
 
     lax.fori_loop(0, heads, finish, 0)
@@ -227,11 +226,18 @@
         wait_bytes(stat_out.at[h], stat_send.at[h])
         wait_bytes(blocks.at[h, pl.ds(0, 10)], out_send.at[h])
         wait_bytes(blocks.at[h, pl.ds(0, 4)], dkv_recv.at[h])
-        wait_bytes(blocks.at[h, pl.ds(0, 4)], dkv_store.at[h])
-        wait_bytes(blocks.at[h, pl.ds(0, 4)], dq_store.at[h])
         return carry
 
     lax.fori_loop(0, heads, drain, 0)
+
+
+def write_out(*refs):
+    sources, targets, sem = refs[:3], refs[3:6], refs[6]
+    copies = [pltpu.make_async_copy(*pair, sem.at[i]) for i, pair in enumerate(zip(sources, targets))]
+    for copy in copies:
+        copy.start()
+    for copy in copies:
+        copy.wait()
 
 
 def solution(mesh):
@@ -244,27 +250,35 @@
         tokens = fh * rh * cols
         quadrant = (fh, rh, cols, HEAD_DIM)
         bf16 = jnp.bfloat16
-        hbm = pl.BlockSpec(memory_space=pl.ANY)
-        out = jax.ShapeDtypeStruct(queries.shape, bf16)
-        return pl.pallas_call(
+        hbm, vmem = pl.BlockSpec(memory_space=pl.ANY), pl.BlockSpec(memory_space=pltpu.VMEM)
+        held = pltpu.VMEM(queries.shape, bf16)
+        grads = pl.pallas_call(
             functools.partial(kernel, tm, rows),
-            out_shape=(out, out, out),
+            out_shape=(held, held, held),
             in_specs=[hbm] * 4,
-            out_specs=(hbm, hbm, hbm),
+            out_specs=(vmem, vmem, vmem),
             scratch_shapes=[
                 pltpu.VMEM((heads, 2 * PER_HALF, *quadrant), bf16),
                 pltpu.VMEM((heads, 2, 2, 4 * tokens), jnp.float32),
                 pltpu.VMEM((heads, 2, 2, 4 * tokens), jnp.float32),
                 pltpu.VMEM((heads, 2, 4, *quadrant), bf16),
-                pltpu.VMEM((heads, 2, 2, 2, *quadrant), bf16),
+                pltpu.VMEM((heads, 2, 2, *quadrant), bf16),
                 pltpu.VMEM((heads, 6, *quadrant), bf16),
-                pltpu.VMEM((heads, 2, 2, *quadrant), bf16),
-                pltpu.SemaphoreType.DMA((10, heads)),
+                pltpu.SemaphoreType.DMA((8, heads)),
             ],
             compiler_params=pltpu.CompilerParams(
-                collective_id=0, has_side_effects=True, vmem_limit_bytes=60 * 1024 * 1024
+                collective_id=0, has_side_effects=True, vmem_limit_bytes=57 * 1024 * 1024
             ),
         )(queries, keys, values, out_grad)
+        out = jax.ShapeDtypeStruct(queries.shape, bf16)
+        return pl.pallas_call(
+            write_out,
+            out_shape=(out, out, out),
+            in_specs=[vmem] * 3,
+            out_specs=(hbm, hbm, hbm),
+            scratch_shapes=[pltpu.SemaphoreType.DMA((3,))],
+            compiler_params=pltpu.CompilerParams(vmem_limit_bytes=4 * 1024 * 1024),
+        )(*(pltpu.with_memory_space_constraint(grad, pltpu.VMEM) for grad in grads))
 
     spec = P("tm", "rows", None, None)
     return jax.shard_map(

time: 142 us -> 138 us (0.972)
  local copies, waits for them, and re-layouts: 6.4 us -> 0 us
  Pallas kernels: 135 us -> 137 us
    unnamed x7 -> x0, local copies, waits for them, and re-layouts: 6.4 us -> none
    pallas_call x1 -> x2, Pallas kernels: 135 us -> 137 us  [the longest x1 135 us: shards(): pl.pallas_call(functools.partial(kernel, tm, rows), out_shape=(held, held...]
where the time goes in v2:
time: 138 us
  Pallas kernels  137 us (99%)
    pallas_call x1, Pallas kernels, shards(): pl.pallas_call(functools.partial(kernel, tm, rows), out_shape=(held, held...  135 us

profile of v2, /device:TPU:4, one launch (start us, length us, event | category | flops | bytes accessed | tf_op | source)
XLA Modules:
  0.0 137.9 jit_solution(15398637317707313294)
XLA Ops:
  0.6 134.8 %shard_map.67 = (bf16[4,8,16,1792]{3,2,1,0:T(8,128)(2,1)S(1)}, bf16[4,8,16,1792]{3,2,1,0:T(8,128)(2,1)S(1)}, bf16[4,8,16,1792]{3,2,1,0:T(8,128)(2,1)S(1)}) custom-call(bf16[4,8,16,1792]{3,2,1,0:T(8,128)(2,1)} %q_ref.1, bf16[4,8,16,1792]{3,2,1,0:T(8,128)(2,1)} %k_ref.1, bf16[4,8,16,1792]{3,2,1,0:T(8,128)(2,1)} %v_ref.1, bf16[4,8,16,1792]{3,2,1,0:T(8,128)(2,1)} %g_ref.1), custom_call_target="tpu_custom_call" | custom-call | tf_op jit(solution)/shard_map/pallas_call | solution.py:255
  135.4 2.5 %shard_map.68 = (bf16[4,8,16,1792]{3,2,1,0:T(8,128)(2,1)}, bf16[4,8,16,1792]{3,2,1,0:T(8,128)(2,1)}, bf16[4,8,16,1792]{3,2,1,0:T(8,128)(2,1)}) custom-call(bf16[4,8,16,1792]{3,2,1,0:T(8,128)(2,1)S(1)} %get-tuple-element.6.refs_0_, bf16[4,8,16,1792]{3,2,1,0:T(8,128)(2,1)S(1)} %get-tuple-element.7.refs_1_, bf16[4,8,16,1792]{3,2,1,0:T(8,128)(2,1)S(1)} %get-tuple-element.8.refs_2_), custom_call_target="tpu_custom_call" | custom-call | tf_op jit(solution)/shard_map/pallas_call | solution.py:274

commit v3 on v2

--- a/solution.py
+++ b/solution.py
@@ -11,8 +11,8 @@
 MESH = pl.DeviceIdType.MESH
 HEAD_DIM = 128
 WW = 8
-AHEAD = 3
-LAG = 3
+AHEAD = 2
+LAG = 5
 
 PER_HALF = 12
 OWN_ROLE = (2, 0)
@@ -56,8 +56,8 @@
         pltpu.make_async_copy(ref, ref, sem).wait()
 
     barrier = pltpu.get_barrier_semaphore()
-    around = [(tp, r), (tn, r), (t, rp), (t, rn), (tp, rp), (tp, rn), (tn, rp), (tn, rn)]
-    for device in around:
+    senders = [(tp, r), (tn, r), (t, rp), (tp, rp), (tn, rp)]
+    for device in senders:
         pl.semaphore_signal(barrier, inc=1, device_id=device, device_id_type=MESH)
 
     def load_own(h, carry):
@@ -69,7 +69,7 @@
         return carry
 
     lax.fori_loop(0, heads, load_own, 0)
-    pl.semaphore_wait(barrier, len(around))
+    pl.semaphore_wait(barrier, len(senders))
 
     def send_inputs(h):
         sem = (fwd_send.at[h], fwd_recv.at[h])
@@ -101,12 +101,12 @@
 
     def send_outputs(h):
         sem = (out_send.at[h], dq_recv.at[h])
+        send(dq_part.at[h, 1, 1], dq_in.at[h, 0], *sem, (t, rp))
+        send(dq_part.at[h, 0, 3], dq_in.at[h, 3], *sem, (t, rp))
+        send(dq_part.at[h, 1, 3], dq_in.at[h, 2], *sem, (tp, rp))
+        send(dq_part.at[h, 0, 1], dq_in.at[h, 1], *sem, (tn, rp))
         send(dq_part.at[h, 1, 2], dq_in.at[h, 5], *sem, (tp, r))
         send(dq_part.at[h, 0, 0], dq_in.at[h, 4], *sem, (tn, r))
-        send(dq_part.at[h, 1, 3], dq_in.at[h, 2], *sem, (tp, rp))
-        send(dq_part.at[h, 0, 1], dq_in.at[h, 1], *sem, (tn, rp))
-        send(dq_part.at[h, 1, 1], dq_in.at[h, 0], *sem, (t, rp))
-        send(dq_part.at[h, 0, 3], dq_in.at[h, 3], *sem, (t, rp))
         sem = (out_send.at[h], dkv_recv.at[h])
         for kind, ref in enumerate((dk_ref, dv_ref)):
             send(dkv.at[h, kind, 1], quad(ref, 1 - seam_after, 0, h), *sem, ((t + seam_after) % tm, rp))
@@ -172,8 +172,13 @@
                 put(ref, half, 1, h, total[0])
                 dkv[h, kind, half] = total[1]
 
-    for h in range(min(AHEAD, heads)):
+    ahead = AHEAD + 2 * (seam_before + seam_after)
+
+    def send_first(h, carry):
         send_inputs(h)
+        return carry
+
+    lax.fori_loop(0, ahead, send_first, 0)
 
     def step(i, carry):
         @pl.when(i < heads)
@@ -181,9 +186,9 @@
             wait_bytes(blocks.at[i, pl.ds(0, 8)], load_sem.at[i])
             wait_bytes(blocks.at[i, pl.ds(0, 16)], fwd_recv.at[i])
 
-        @pl.when(i + AHEAD < heads)
-        def _():
-            send_inputs(i + AHEAD)
+        @pl.when(i + ahead < heads)
+        def _():
+            send_inputs(i + ahead)
 
         @pl.when(i > LAG)
         def _():
@@ -233,7 +238,11 @@
 
 def write_out(*refs):
     sources, targets, sem = refs[:3], refs[3:6], refs[6]
-    copies = [pltpu.make_async_copy(*pair, sem.at[i]) for i, pair in enumerate(zip(sources, targets))]
+    copies = [
+        pltpu.make_async_copy(source.at[frame], target.at[frame], sem.at[i, frame])
+        for i, (source, target) in enumerate(zip(sources, targets))
+        for frame in range(source.shape[0])
+    ]
     for copy in copies:
         copy.start()
     for copy in copies:
@@ -276,7 +285,7 @@
             out_shape=(out, out, out),
             in_specs=[vmem] * 3,
             out_specs=(hbm, hbm, hbm),
-            scratch_shapes=[pltpu.SemaphoreType.DMA((3,))],
+            scratch_shapes=[pltpu.SemaphoreType.DMA((3, frames))],
             compiler_params=pltpu.CompilerParams(vmem_limit_bytes=4 * 1024 * 1024),
         )(*(pltpu.with_memory_space_constraint(grad, pltpu.VMEM) for grad in grads))
 

time: 138 us -> 135 us (0.978)
  Pallas kernels: 137 us -> 134 us
    pallas_call x1, Pallas kernels: 135 us -> 131 us  [shards(): pl.pallas_call(functools.partial(kernel, tm, rows), out_shape=(held, held...]
where the time goes in v3:
time: 135 us
  Pallas kernels  134 us (99%)
    pallas_call x1, Pallas kernels, shards(): pl.pallas_call(functools.partial(kernel, tm, rows), out_shape=(held, held...  131 us

profile of v3, /device:TPU:4, one launch (start us, length us, event | category | flops | bytes accessed | tf_op | source)
XLA Modules:
  0.0 134.7 jit_solution(2779710280512275676)
XLA Ops:
  0.6 131.5 %shard_map.67 = (bf16[4,8,16,1792]{3,2,1,0:T(8,128)(2,1)S(1)}, bf16[4,8,16,1792]{3,2,1,0:T(8,128)(2,1)S(1)}, bf16[4,8,16,1792]{3,2,1,0:T(8,128)(2,1)S(1)}) custom-call(bf16[4,8,16,1792]{3,2,1,0:T(8,128)(2,1)} %q_ref.1, bf16[4,8,16,1792]{3,2,1,0:T(8,128)(2,1)} %k_ref.1, bf16[4,8,16,1792]{3,2,1,0:T(8,128)(2,1)} %v_ref.1, bf16[4,8,16,1792]{3,2,1,0:T(8,128)(2,1)} %g_ref.1), custom_call_target="tpu_custom_call" | custom-call | tf_op jit(solution)/shard_map/pallas_call | solution.py:264
  132.1 2.5 %shard_map.68 = (bf16[4,8,16,1792]{3,2,1,0:T(8,128)(2,1)}, bf16[4,8,16,1792]{3,2,1,0:T(8,128)(2,1)}, bf16[4,8,16,1792]{3,2,1,0:T(8,128)(2,1)}) custom-call(bf16[4,8,16,1792]{3,2,1,0:T(8,128)(2,1)S(1)} %get-tuple-element.6.refs_0_, bf16[4,8,16,1792]{3,2,1,0:T(8,128)(2,1)S(1)} %get-tuple-element.7.refs_1_, bf16[4,8,16,1792]{3,2,1,0:T(8,128)(2,1)S(1)} %get-tuple-element.8.refs_2_), custom_call_target="tpu_custom_call" | custom-call | tf_op jit(solution)/shard_map/pallas_call | solution.py:283

commit v4 on v3

--- a/solution.py
+++ b/solution.py
@@ -29,6 +29,7 @@
     seam_before = 1 - (r % side + side - 1) // side
     seam_after = 1 - ((r + 1) % side + side - 1) // side
     tp, tn = (t + 1) % tm, (t + tm - 1) % tm
+    first_way = (t + 1) // tm
     rp, rn = (r + 1) % rows, (r + rows - 1) % rows
 
     (fwd_send, fwd_recv, load_sem, stat_send, stat_recv, out_send, dq_recv, dkv_recv) = (
@@ -103,10 +104,10 @@
         sem = (out_send.at[h], dq_recv.at[h])
         send(dq_part.at[h, 1, 1], dq_in.at[h, 0], *sem, (t, rp))
         send(dq_part.at[h, 0, 3], dq_in.at[h, 3], *sem, (t, rp))
-        send(dq_part.at[h, 1, 3], dq_in.at[h, 2], *sem, (tp, rp))
-        send(dq_part.at[h, 0, 1], dq_in.at[h, 1], *sem, (tn, rp))
-        send(dq_part.at[h, 1, 2], dq_in.at[h, 5], *sem, (tp, r))
-        send(dq_part.at[h, 0, 0], dq_in.at[h, 4], *sem, (tn, r))
+        for way in (first_way, 1 - first_way):
+            beside = (t + tm + 2 * way - 1) % tm
+            send(dq_part.at[h, way, 1 + 2 * way], dq_in.at[h, 1 + way], *sem, (beside, rp))
+            send(dq_part.at[h, way, 2 * way], dq_in.at[h, 4 + way], *sem, (beside, r))
         sem = (out_send.at[h], dkv_recv.at[h])
         for kind, ref in enumerate((dk_ref, dv_ref)):
             send(dkv.at[h, kind, 1], quad(ref, 1 - seam_after, 0, h), *sem, ((t + seam_after) % tm, rp))

time: 135 us -> 135 us (level)
  no operation moved by 1% of the time
where the time goes in v4:
time: 135 us
  Pallas kernels  134 us (99%)
    pallas_call x1, Pallas kernels, shards(): pl.pallas_call(functools.partial(kernel, tm, rows), out_shape=(held, held...  131 us

profile of v4, /device:TPU:4, one launch (start us, length us, event | category | flops | bytes accessed | tf_op | source)
XLA Modules:
  0.0 134.7 jit_solution(1509563860913259399)
XLA Ops:
  0.6 131.5 %shard_map.67 = (bf16[4,8,16,1792]{3,2,1,0:T(8,128)(2,1)S(1)}, bf16[4,8,16,1792]{3,2,1,0:T(8,128)(2,1)S(1)}, bf16[4,8,16,1792]{3,2,1,0:T(8,128)(2,1)S(1)}) custom-call(bf16[4,8,16,1792]{3,2,1,0:T(8,128)(2,1)} %q_ref.1, bf16[4,8,16,1792]{3,2,1,0:T(8,128)(2,1)} %k_ref.1, bf16[4,8,16,1792]{3,2,1,0:T(8,128)(2,1)} %v_ref.1, bf16[4,8,16,1792]{3,2,1,0:T(8,128)(2,1)} %g_ref.1), custom_call_target="tpu_custom_call" | custom-call | tf_op jit(solution)/shard_map/pallas_call | solution.py:265
  132.1 2.5 %shard_map.68 = (bf16[4,8,16,1792]{3,2,1,0:T(8,128)(2,1)}, bf16[4,8,16,1792]{3,2,1,0:T(8,128)(2,1)}, bf16[4,8,16,1792]{3,2,1,0:T(8,128)(2,1)}) custom-call(bf16[4,8,16,1792]{3,2,1,0:T(8,128)(2,1)S(1)} %get-tuple-element.6.refs_0_, bf16[4,8,16,1792]{3,2,1,0:T(8,128)(2,1)S(1)} %get-tuple-element.7.refs_1_, bf16[4,8,16,1792]{3,2,1,0:T(8,128)(2,1)S(1)} %get-tuple-element.8.refs_2_), custom_call_target="tpu_custom_call" | custom-call | tf_op jit(solution)/shard_map/pallas_call | solution.py:284
